TPU v7x, 256 devices: a whole 4x4x8 slice. The times are simulated.
256 devices in a mesh: seq: 64 (over z, x, core), head: 4 (over y).
Axes of the slice: x: 4, y: 4, z: 8, core: 2. Of those that a mesh axis runs over, the one named last changes fastest.
Arguments:
- tokens: bfloat16 [65536, 2048], P('seq', 'head'), may hold values from -8 to 8
- w_query: bfloat16 [2048, 2048], P(None, 'head'), may hold values from -1 to 1, as said below
- w_key: bfloat16 [2048, 2048], P(None, 'head'), may hold values from -1 to 1, as said below
- w_value: bfloat16 [2048, 2048], P(None, 'head'), may hold values from -0.125 to 0.125
- w_out: bfloat16 [2048, 2048], P('head'), may hold values from -0.125 to 0.125
- mix_logit: float32 [8], P('head'), may hold values from -2 to 2
Outputs:
- layer_out: bfloat16 [65536, 2048], P('seq', 'head')
Inputs may be any that keep to these rules, and one draw needn't show every extreme that they name: `w_query`: entries of mean zero with a standard deviation of about 2048 ** -0.5. `w_key`: entries of mean zero with a standard deviation of about 2048 ** -0.5.
All inputs are finite; a program needn't handle non-finite values.
Results may differ from a plain program's by a relative error of at most 0.0065.
Values may be sent and summed in bfloat16 or wider, within the bound.
A program may use at most 128 MiB of HBM per device.

v0:
```python
import jax
import jax.numpy as jnp
from jax import lax
from jax.sharding import Mesh
from jax.sharding import PartitionSpec as P

SEQ = ("seq_0", "seq_1", "seq_2")


def nothing_yet(shard, identity):
    return jax.tree.map(
        lambda a, e: jnp.broadcast_to(jnp.asarray(e, a.dtype), a.shape), shard, identity
    )


def carried_in(shard, axes, combine, identity):
    before = start = nothing_yet(shard, identity)
    running = shard
    for axis in reversed(axes):
        length, mine = (lax.axis_size(axis), lax.axis_index(axis))
        pieces = jax.tree.map(
            lambda part, kind: lax.all_gather(part.astype(kind), axis),
            running,
            (jnp.bfloat16, jnp.bfloat16),
        )
        inside, running = (start, start)
        for k in range(length):
            passed = k < mine
            running = combine(
                running, jax.tree.map(lambda part, own: part[k].astype(own.dtype), pieces, shard)
            )
            inside = jax.tree.map(lambda new, old: jnp.where(passed, new, old), running, inside)
        before = combine(inside, before)
    return before


def feature(values):
    return jax.nn.elu(values) + 1.0


def add_pairs(earlier, later):
    return (earlier[0] + later[0], earlier[1] + later[1])


def on_device(tokens, w_query, w_key, w_value, w_out, mix_logit):
    seg = tokens.shape[0]
    heads = mix_logit.shape[0]
    width = w_query.shape[1]
    hsize = width // heads
    empty = jnp.zeros((seg, width), jnp.float32)
    totals = (empty, empty, empty)
    piece = lax.all_gather(tokens, "head", axis=1, tiled=True)
    result = []
    for total, weight in zip(totals, (w_query, w_key, w_value)):
        result.append(jnp.dot(piece, weight, preferred_element_type=jnp.float32))
    query, keys, values = tuple(result)
    query = query.astype(jnp.bfloat16).reshape(seg, heads, hsize)
    keys = keys.astype(jnp.bfloat16).reshape(seg, heads, hsize)
    values = values.astype(jnp.bfloat16).reshape(seg, heads, hsize)
    fkey = feature(keys.astype(jnp.float32)).astype(jnp.bfloat16)
    mem_term = jnp.einsum("thd,the->hde", fkey, values, preferred_element_type=jnp.float32)
    norm_term = jnp.sum(fkey.astype(jnp.float32), axis=0)
    zeros_pair = (jnp.zeros_like(mem_term), jnp.zeros_like(norm_term))
    memory, normal = carried_in((mem_term, norm_term), SEQ, add_pairs, zeros_pair)
    rows = lax.broadcasted_iota(jnp.int32, (seg, seg), 0)
    cols = lax.broadcasted_iota(jnp.int32, (seg, seg), 1)
    causal = cols <= rows
    scale = 1.0 / hsize**0.5
    scores = jnp.einsum("qhd,khd->hqk", query, keys, preferred_element_type=jnp.float32) * scale
    scores = jnp.where(causal[None], scores, -1e30)
    expo = jnp.exp(scores - jnp.max(scores, axis=2, keepdims=True))
    probs = (expo / jnp.sum(expo, axis=2, keepdims=True)).astype(jnp.bfloat16)
    local = jnp.einsum("hqk,khd->qhd", probs, values, preferred_element_type=jnp.float32)
    fquery = feature(query.astype(jnp.float32)).astype(jnp.bfloat16).astype(jnp.float32)
    numer = jnp.einsum("thd,hde->the", fquery, memory, precision=lax.Precision.HIGHEST)
    denom = jnp.einsum("thd,hd->th", fquery, normal, precision=lax.Precision.HIGHEST)
    readout = numer / jnp.maximum(denom, 1.0)[:, :, None]
    share = jax.nn.sigmoid(mix_logit)[None, :, None]
    mixed = (share * readout + (1.0 - share) * local).astype(jnp.bfloat16).reshape(seg, width)
    columns = lax.all_to_all(w_out, "head", split_axis=1, concat_axis=0, tiled=True)
    summed = jnp.dot(
        lax.all_gather(mixed, "head", axis=1, tiled=True),
        columns,
        preferred_element_type=jnp.float32,
    )
    return summed.astype(jnp.bfloat16)


def solution(mesh):
    torus = Mesh(
        mesh.devices.reshape(8, 4, 2, mesh.shape["head"]), ("seq_0", "seq_1", "seq_2", "head")
    )
    return jax.shard_map(
        on_device,
        mesh=torus,
        in_specs=(
            P(SEQ, "head"),
            P(None, "head"),
            P(None, "head"),
            P(None, "head"),
            P("head", None),
            P("head"),
        ),
        out_specs=P(SEQ, "head"),
        check_vma=False,
    )
```

profile of v0, /device:TPU:1, one launch (start us, length us, event | category | flops | bytes accessed | tf_op | source)
XLA Modules:
  0.0 251.1 jit_solution(9462103053753191697)
XLA Ops:
  6.5 0.0 copy-start
  6.5 0.0 all-gather.6.cloned.1.call-start
  6.5 0.7 all-gather.6.cloned.1.call-update
  7.3 0.0 all-gather.8.cloned.1.call-start
  7.3 56.3 %all-gather.6.cloned.1.call-done = bf16[1024,2048]{1,0:T(8,128)(2,1)} async-done(((bf16[1024,512]{1,0:T(8,128)(2,1)}), bf16[1024,2048]{1,0:T(8,128)(2,1)}) %all-gather.6.cloned.1.call-update) | async-done | bytes 4194320 | tf_op jit(solution)/shard_map/all_gather | solution.py:52
  63.6 0.0 copy-done
  63.6 6.2 %fusion.20 = (bf16[512]{0:T(512)(128)(2,1)S(1)}, bf16[1024,512]{0,1:T(8,128)(2,1)}) fusion(bf16[1024,2048]{1,0:T(8,128)(2,1)} %all-gather.6.cloned.1.call-done, bf16[2048,512]{1,0:T(8,128)(2,1)S(1)} %copy-done), kind=kOutput, calls=%fused_computation.36 | convolution fusion | flops 2151677440 | bytes 7341056 | tf_op jit(solution)/shard_map/dot_general | solution.py:55
  69.8 2.3 copy.33
  72.1 0.0 copy-start.1
  72.1 5.3 %convolution_convert_fusion.2 = bf16[1024,512]{0,1:T(8,128)(2,1)S(1)} fusion(bf16[1024,2048]{1,0:T(8,128)(2,1)} %all-gather.6.cloned.1.call-done, bf16[2048,512]{1,0:T(8,128)(2,1)} %param.9), kind=kOutput, calls=%fused_computation.31 | convolution fusion | flops 2148007936 | bytes 7340032 | tf_op jit(solution)/shard_map/dot_general | solution.py:55
  77.4 0.0 copy-start.3
  77.4 0.0 copy-done.1
  77.4 0.0 copy-start.2
  77.4 1.2 convolution_convert_fusion.4
  78.7 0.0 copy-done.3
  78.7 2.7 %all-gather = bf16[4,256,256]{2,1,0:T(8,128)(2,1)S(1)} all-gather(bf16[2,256,256]{2,1,0:T(8,128)(2,1)S(1)} %convolution_convert_fusion.4), channel_id=2, replica_groups=mesh['seq_0'=8,'seq_1'=4,'seq_2'=2,'head'=4] {'seq_2'}, dimensions={0}, use_global_device_ids=true | all-gather | bytes 786432 | tf_op jit(solution)/shard_map/all_gather | solution.py:22
  81.3 0.8 fusion.59
  82.1 0.0 all-gather.8.cloned.1.call-update
  82.1 0.0 all-gather.10.cloned.1.call-start
  82.2 0.0 copy-done.2
  82.2 24.7 %all-gather.8.cloned.1.call-done = bf16[4,2,256,256]{3,2,1,0:T(8,128)(2,1)} async-done(((bf16[1,2,256,256]{3,2,1,0:T(8,128)(2,1)}), bf16[4,2,256,256]{3,2,1,0:T(8,128)(2,1)}) %all-gather.8.cloned.1.call-update) | async-done | bytes 1048592 | tf_op jit(solution)/shard_map/all_gather | solution.py:22
  106.9 2.0 fusion.55
  108.9 0.0 all-gather.10.cloned.1.call-update
  108.9 0.0 all-gather.12.cloned.1.call-start
  109.0 1.3 iota_compare_fusion
  110.3 6.2 %convolution_convert_fusion.1 = bf16[1024,512]{0,1:T(8,128)(2,1)} fusion(bf16[1024,2048]{1,0:T(8,128)(2,1)} %all-gather.6.cloned.1.call-done, bf16[2048,512]{1,0:T(8,128)(2,1)} %param.7), kind=kOutput, calls=%fused_computation.30 | convolution fusion | flops 2148007936 | bytes 7340032 | tf_op jit(solution)/shard_map/dot_general | solution.py:55
  116.5 2.3 copy.36
  118.8 4.2 %all_gather.40 = bf16[2,2,256]{2,1,0:T(2,128)(2,1)S(1)} all-gather(bf16[1,2,256]{2,1,0:T(2,128)(2,1)S(1)} %all_gather.39), channel_id=1, replica_groups=mesh['seq_0'=8,'seq_1'=4,'seq_2'=2,'head'=4] {'seq_2'}, dimensions={0}, use_global_device_ids=true | all-gather | bytes 3072 | tf_op jit(solution)/shard_map/all_gather | solution.py:22
  123.0 6.7 %all_gather.41 = bf16[4,2,256]{2,1,0:T(2,128)(2,1)S(1)} all-gather(bf16[1,2,256]{2,1,0:T(2,128)(2,1)S(1)} %fusion.106), channel_id=1, replica_groups=mesh['seq_0'=8,'seq_1'=4,'seq_2'=2,'head'=4] {'seq_1'}, dimensions={0}, use_global_device_ids=true | all-gather | bytes 5120 | tf_op jit(solution)/shard_map/all_gather | solution.py:22
  129.7 14.9 %all_gather.42 = bf16[8,2,256]{2,1,0:T(2,128)(2,1)S(1)} all-gather(bf16[1,2,256]{2,1,0:T(2,128)(2,1)S(1)} %fusion.105), channel_id=1, replica_groups=mesh['seq_0'=8,'seq_1'=4,'seq_2'=2,'head'=4] {'seq_0'}, dimensions={0}, use_global_device_ids=true | all-gather | bytes 9216 | tf_op jit(solution)/shard_map/all_gather | solution.py:22
  144.6 2.8 %fusion.56 = f32[2,1,1024]{2,1,0:T(1,128)S(1)} fusion(bf16[1024,2,256]{2,0,1:T(8,128)(2,1)} %copy.36, f32[2,256,1]{1,0,2:T(2,128)S(1)} %fusion.94), kind=kOutput, calls=%fused_computation.76 | convolution fusion | flops 9437184 | bytes 1058816 | tf_op jit(solution)/shard_map/thd,hd->th/dot_general | solution.py:76
  147.4 8.4 %fusion.115 = (f32[2,1024]{1,0:T(2,128)S(1)}, f32[2,1024,1024]{1,2,0:T(8,128)}) fusion(pred[1024,1024]{0,1:T(8,128)(4,1)} %iota_compare_fusion, bf16[1024,2,256]{0,2,1:T(8,128)(2,1)} %bitcast.57, bf16[1024,2,256]{0,2,1:T(8,128)(2,1)} %bitcast.54), kind=kOutput, calls=%fused_computation.145 | convolution fusion | flops 1082131456 | bytes 11542528 | tf_op jit(solution)/shard_map/sub | solution.py:71
  155.8 6.3 %fusion.4 = f32[2,256,1024]{2,1,0:T(8,128)} fusion(bf16[1024,2,256]{0,2,1:T(8,128)(2,1)} %bitcast.59, f32[2,1024,1024]{1,2,0:T(8,128)} %get-tuple-element.8, f32[2,1024]{1,0:T(2,128)S(1)} %get-tuple-element.7), kind=kOutput, calls=%fused_computation.14 | convolution fusion | flops 1077936128 | bytes 11542528 | tf_op jit(solution)/shard_map/hqk,khd->qhd/dot_general | solution.py:73
  162.1 0.0 all-gather.10.cloned.1.call-done
  162.1 7.4 %fusion.15 = bf16[1024,2,256]{0,2,1:T(8,128)(2,1)} fusion(f32[2,256,1024]{2,1,0:T(8,128)} %fusion.4, f32[2]{0:T(128)S(1)} %get-tuple-element.5, f32[1024,2]{0,1:T(2,128)S(1)} %fusion.90, f32[2]{0:T(128)S(1)} %get-tuple-element.6, bf16[1024,2,256]{2,0,1:T(8,128)(2,1)} %copy.36, bf16[8,2,256,256]{3,2,1,0:T(8,128)(2,1)} %all-gather.10.cloned.1.call-done, ...), kind=kOutput, calls=%fused_computation.26 | convolution fusion | flops 1621753856 | bytes 7872542 | tf_op jit(solution)/shard_map/thd,hde->the/dot_general | solution.py:75
  169.5 0.0 all-gather.12.cloned.1.call-update
  169.5 4.0 %copy.41 = bf16[512,2048]{0,1:T(8,128)(2,1)} copy(bf16[512,2048]{1,0:T(8,128)(2,1)} %param.10) | data formatting | bytes 4194304 | tf_op args[4]
  173.5 39.7 %all_to_all.19 = bf16[512,4,512]{0,2,1:T(8,128)(2,1)} all-to-all(bf16[512,4,512]{0,2,1:T(8,128)(2,1)} %bitcast.51), channel_id=1, replica_groups=mesh['seq_0'=8,'seq_1'=4,'seq_2'=2,'head'=4] {'head'}, dimensions={1} | all-to-all | bytes 4194304 | tf_op jit(solution)/shard_map/all_to_all | solution.py:80
  213.2 4.2 %copy.42 = bf16[4,512,512]{2,1,0:T(8,128)(2,1)} copy(bf16[4,512,512]{1,2,0:T(8,128)(2,1)} %bitcast.50) | data formatting | bytes 4194304 | tf_op jit(solution)/shard_map/all_to_all | solution.py:80
  217.4 21.0 %all-gather.12.cloned.1.call-done = bf16[1024,2048]{0,1:T(8,128)(2,1)} async-done(((bf16[1024,512]{0,1:T(8,128)(2,1)}), bf16[1024,2048]{0,1:T(8,128)(2,1)}) %all-gather.12.cloned.1.call-update) | async-done | bytes 4194320 | tf_op jit(solution)/shard_map/all_gather | solution.py:82
  238.4 6.2 %convolution_convert_fusion = bf16[1024,512]{1,0:T(8,128)(2,1)} fusion(bf16[1024,2048]{0,1:T(8,128)(2,1)} %all-gather.12.cloned.1.call-done, bf16[2048,512]{1,0:T(8,128)(2,1)} %bitcast.52), kind=kOutput, calls=%fused_computation.29 | convolution fusion | flops 2148007936 | bytes 7340032 | tf_op jit(solution)/shard_map/dot_general | solution.py:81
  (6 shorter events, 0.1 us)
Async XLA Ops:
  6.5 57.0 %copy-start = (bf16[2048,512]{1,0:T(8,128)(2,1)S(1)}, bf16[2048,512]{1,0:T(8,128)(2,1)}, u32[]{:S(2)}) copy-start(bf16[2048,512]{1,0:T(8,128)(2,1)} %param.8) | copy-start | bytes 6291460
  6.5 57.0 %all-gather.6.cloned.1.call-start = ((), (), s32[]{:S(2)}) async-start(), calls=%async_computation.1 | async-start | bytes 5242880 | tf_op jit(solution)/shard_map/all_gather | solution.py:52
  7.3 99.6 %all-gather.8.cloned.1.call-start = ((), (), s32[]{:S(2)}) async-start(), calls=%async_computation.2 | async-start | bytes 1310720 | tf_op jit(solution)/shard_map/all_gather | solution.py:22
  72.1 5.3 %copy-start.1 = (bf16[1024,2,256]{2,0,1:T(8,128)(2,1)S(1)}, bf16[1024,2,256]{2,0,1:T(8,128)(2,1)}, u32[]{:S(2)}) copy-start(bf16[1024,2,256]{2,0,1:T(8,128)(2,1)} %copy.33) | copy-start | bytes 3145732
  77.4 1.3 copy-start.3
  77.4 4.8 %copy-start.2 = (f32[2]{0:T(128)S(1)}, f32[2]{0:T(128)}, u32[]{:S(2)}) copy-start(f32[2]{0:T(128)} %param.11) | copy-start | bytes 28
  82.1 80.0 %all-gather.10.cloned.1.call-start = ((), (), s32[]{:S(2)}) async-start(), calls=%async_computation.3 | async-start | bytes 2359296 | tf_op jit(solution)/shard_map/all_gather | solution.py:22
  108.9 129.4 %all-gather.12.cloned.1.call-start = ((), (), s32[]{:S(2)}) async-start(), calls=%async_computation.4 | async-start | bytes 5242880 | tf_op jit(solution)/shard_map/all_gather | solution.py:82
Sparse Core Ops, SparseCore 0:
  9.1 54.3 all-gather.5
  82.2 24.5 all-gather.7
  109.0 39.1 all-gather.9
  169.6 68.6 all-gather.11
where the time goes:
time: 252 us; the launch traced here: 251 us
  waiting for transfers between devices  103 us (41%)
  blocking collectives  68.1 us (27%)
  matrix products  50.1 us (20%)
  between operations  13.2 us (5%)
  local copies, waits for them, and re-layouts  12.8 us (5%)
  other arithmetic  4.18 us (2%)
    all_gather x1, waiting for transfers between devices, on_device(): piece = lax.all_gather(tokens, 'head', axis=1, tiled=True)  56.3 us
    all_to_all x1, blocking collectives, on_device(): lax.all_to_all(w_out, 'head', split_axis=1, concat_axis=0, tiled=True)  39.7 us
    all_gather x4, blocking collectives, carried_in(): lax.all_gather(part.astype(kind), axis)  28.4 us
    all_gather x2, waiting for transfers between devices, carried_in(): lax.all_gather(part.astype(kind), axis)  24.7 us
    all_gather x1, waiting for transfers between devices, on_device(): lax.all_gather(mixed, 'head', axis=1, tiled=True)  21 us
    dot_general x3, matrix products, on_device(): result.append(jnp.dot(piece, weight, preferred_element_type=jnp.float32))  17.7 us
    sub x1, matrix products, on_device(): expo = jnp.exp(scores - jnp.max(scores, axis=2, keepdims=True))  8.38 us
    dot_general x1, matrix products, on_device(): jnp.einsum('thd,hde->the', fquery, memory, precision=lax.Precision.HIGHEST)  7.36 us
  transfers between devices with their start and end apart: 4, of which 3 were waited for; matrix products, arithmetic and copies ran while one was open for 14% of the time, Pallas kernels for 0%

commit v1 on v0

--- a/solution.py
+++ b/solution.py
@@ -49,7 +49,9 @@
     hsize = width // heads
     empty = jnp.zeros((seg, width), jnp.float32)
     totals = (empty, empty, empty)
-    piece = lax.all_gather(tokens, "head", axis=1, tiled=True)
+    piece = jnp.concatenate(
+        lax.all_to_all(jnp.stack([tokens] * lax.axis_size("head")), "head", 0, 0), 1
+    )
     result = []
     for total, weight in zip(totals, (w_query, w_key, w_value)):
         result.append(jnp.dot(piece, weight, preferred_element_type=jnp.float32))

time: 252 us -> 247 us (0.980)
  waiting for transfers between devices: 103 us -> 45.9 us
  blocking collectives: 68.1 us -> 122 us
  matrix products: 50.1 us -> 46.6 us
    all_gather x1 -> x0, waiting for transfers between devices: 56.3 us -> none  [on_device(): piece = lax.all_gather(tokens, 'head', axis=1, tiled=True)]
    all_to_all x0 -> x1, blocking collectives: none -> 52.9 us  [on_device(): lax.all_to_all(jnp.stack([tokens] * lax.axis_size('head')), 'head', 0, 0)]
    dot_general x3, matrix products: 17.7 us -> 12.8 us  [on_device(): result.append(jnp.dot(piece, weight, preferred_element_type=jnp.float32))]
    unnamed x9 -> x12, local copies, waits for them, and re-layouts: 4.01 us -> 5.64 us
  transfers between devices with their start and end apart: 4 -> 3, of which waited for: 3 -> 2; matrix products, arithmetic and copies ran while one was open for 14% -> 14% of each run, Pallas kernels for 0% -> 0%
where the time goes in v1:
time: 247 us; the launch traced here: 246 us
  blocking collectives  122 us (49%)
  matrix products  46.6 us (19%)
  waiting for transfers between devices  45.9 us (19%)
  local copies, waits for them, and re-layouts  14 us (6%)
  between operations  13.2 us (5%)
  other arithmetic  4.16 us (2%)
    all_to_all x1, blocking collectives, on_device(): lax.all_to_all(jnp.stack([tokens] * lax.axis_size('head')), 'head', 0, 0)  52.9 us
    all_to_all x1, blocking collectives, on_device(): lax.all_to_all(w_out, 'head', split_axis=1, concat_axis=0, tiled=True)  40.1 us
    all_gather x4, blocking collectives, carried_in(): lax.all_gather(part.astype(kind), axis)  29.4 us
    all_gather x2, waiting for transfers between devices, carried_in(): lax.all_gather(part.astype(kind), axis)  25.3 us
    all_gather x1, waiting for transfers between devices, on_device(): lax.all_gather(mixed, 'head', axis=1, tiled=True)  20.6 us
    dot_general x3, matrix products, on_device(): result.append(jnp.dot(piece, weight, preferred_element_type=jnp.float32))  12.8 us
    sub x1, matrix products, on_device(): expo = jnp.exp(scores - jnp.max(scores, axis=2, keepdims=True))  8.39 us
    dot_general x1, matrix products, on_device(): jnp.einsum('thd,hde->the', fquery, memory, precision=lax.Precision.HIGHEST)  7.36 us
  transfers between devices with their start and end apart: 3, of which 2 were waited for; matrix products, arithmetic and copies ran while one was open for 14% of the time, Pallas kernels for 0%

profile of v1, /device:TPU:1, one launch (start us, length us, event | category | flops | bytes accessed | tf_op | source)
XLA Modules:
  0.0 246.3 jit_solution(4145251127590926697)
XLA Ops:
  6.5 0.0 copy-start
  6.5 0.0 all-gather.5.cloned.1.call-start
  6.5 1.6 copy.35
  8.2 0.5 stack.2
  8.7 0.0 copy-start.3
  8.7 52.9 %all_to_all.24 = bf16[4,1024,512]{1,2,0:T(8,128)(2,1)S(1)} all-to-all(bf16[4,1024,512]{1,2,0:T(8,128)(2,1)S(1)} %stack.2), channel_id=1, replica_groups=mesh['seq_0'=8,'seq_1'=4,'seq_2'=2,'head'=4] {'head'}, dimensions={0} | all-to-all | bytes 8388608 | tf_op jit(solution)/shard_map/all_to_all | solution.py:53
  61.6 0.0 copy-start.1
  61.6 0.0 copy-done.3
  61.6 3.4 %convolution_convert_fusion.2 = bf16[1024,512]{0,1:T(8,128)(2,1)} fusion(bf16[1024,2048]{0,1:T(8,128)(2,1)S(1)} %bitcast.55, bf16[2048,512]{1,0:T(8,128)(2,1)S(1)} %copy-done.3), kind=kOutput, calls=%fused_computation.31 | convolution fusion | flops 2148007936 | bytes 7340032 | tf_op jit(solution)/shard_map/dot_general | solution.py:57
  65.0 0.0 copy-done.1
  65.0 0.0 copy-done
  65.0 3.2 %fusion.20 = (bf16[512]{0:T(512)(128)(2,1)S(1)}, bf16[1024,512]{0,1:T(8,128)(2,1)S(1)}) fusion(bf16[1024,2048]{0,1:T(8,128)(2,1)S(1)} %bitcast.56, bf16[2048,512]{1,0:T(8,128)(2,1)S(1)} %copy-done), kind=kOutput, calls=%fused_computation.36 | convolution fusion | flops 2151677440 | bytes 7341056 | tf_op jit(solution)/shard_map/dot_general | solution.py:57
  68.2 0.0 copy-start.2
  68.2 1.4 copy.36
  69.5 0.0 copy-done.2
  69.5 0.0 copy-start.4
  69.5 2.8 %convolution_convert_fusion.4 = bf16[2,256,256]{2,1,0:T(8,128)(2,1)S(1)} fusion(bf16[1024,2,256]{0,2,1:T(8,128)(2,1)} %bitcast.64, bf16[1024,2,256]{2,0,1:T(8,128)(2,1)} %copy.36), kind=kOutput, calls=%fused_computation.33 | convolution fusion | flops 271712256 | bytes 2359296 | tf_op jit(solution)/shard_map/thd,the->hde/dot_general | solution.py:63
  72.3 3.6 %all-gather = bf16[4,256,256]{2,1,0:T(8,128)(2,1)S(1)} all-gather(bf16[2,256,256]{2,1,0:T(8,128)(2,1)S(1)} %convolution_convert_fusion.4), channel_id=2, replica_groups=mesh['seq_0'=8,'seq_1'=4,'seq_2'=2,'head'=4] {'seq_2'}, dimensions={0}, use_global_device_ids=true | all-gather | bytes 786432 | tf_op jit(solution)/shard_map/all_gather | solution.py:22
  76.0 0.8 fusion.59
  76.7 0.0 all-gather.5.cloned.1.call-update
  76.8 0.0 all-gather.7.cloned.1.call-start
  76.8 0.0 copy-done.4
  76.8 25.3 %all-gather.5.cloned.1.call-done = bf16[4,2,256,256]{3,2,1,0:T(8,128)(2,1)} async-done(((bf16[1,2,256,256]{3,2,1,0:T(8,128)(2,1)}), bf16[4,2,256,256]{3,2,1,0:T(8,128)(2,1)}) %all-gather.5.cloned.1.call-update) | async-done | bytes 1048592 | tf_op jit(solution)/shard_map/all_gather | solution.py:22
  102.1 2.0 fusion.55
  104.1 0.0 all-gather.7.cloned.1.call-update
  104.2 0.0 all-gather.9.cloned.1.call-start
  104.2 1.3 iota_compare_fusion
  105.5 6.2 %convolution_convert_fusion.1 = bf16[1024,512]{0,1:T(8,128)(2,1)} fusion(bf16[1024,2048]{0,1:T(8,128)(2,1)} %bitcast.57, bf16[2048,512]{1,0:T(8,128)(2,1)} %param.7), kind=kOutput, calls=%fused_computation.30 | convolution fusion | flops 2148007936 | bytes 7340032 | tf_op jit(solution)/shard_map/dot_general | solution.py:57
  111.7 2.2 copy.39
  114.0 4.2 %all_gather.36 = bf16[2,2,256]{2,1,0:T(2,128)(2,1)S(1)} all-gather(bf16[1,2,256]{2,1,0:T(2,128)(2,1)S(1)} %all_gather.35), channel_id=1, replica_groups=mesh['seq_0'=8,'seq_1'=4,'seq_2'=2,'head'=4] {'seq_2'}, dimensions={0}, use_global_device_ids=true | all-gather | bytes 3072 | tf_op jit(solution)/shard_map/all_gather | solution.py:22
  118.2 6.7 %all_gather.37 = bf16[4,2,256]{2,1,0:T(2,128)(2,1)S(1)} all-gather(bf16[1,2,256]{2,1,0:T(2,128)(2,1)S(1)} %fusion.106), channel_id=1, replica_groups=mesh['seq_0'=8,'seq_1'=4,'seq_2'=2,'head'=4] {'seq_1'}, dimensions={0}, use_global_device_ids=true | all-gather | bytes 5120 | tf_op jit(solution)/shard_map/all_gather | solution.py:22
  124.9 14.9 %all_gather.38 = bf16[8,2,256]{2,1,0:T(2,128)(2,1)S(1)} all-gather(bf16[1,2,256]{2,1,0:T(2,128)(2,1)S(1)} %fusion.105), channel_id=1, replica_groups=mesh['seq_0'=8,'seq_1'=4,'seq_2'=2,'head'=4] {'seq_0'}, dimensions={0}, use_global_device_ids=true | all-gather | bytes 9216 | tf_op jit(solution)/shard_map/all_gather | solution.py:22
  139.8 2.8 %fusion.56 = f32[2,1,1024]{2,1,0:T(1,128)S(1)} fusion(bf16[1024,2,256]{2,0,1:T(8,128)(2,1)} %copy.39, f32[2,256,1]{1,0,2:T(2,128)S(1)} %fusion.94), kind=kOutput, calls=%fused_computation.76 | convolution fusion | flops 9437184 | bytes 1058816 | tf_op jit(solution)/shard_map/thd,hd->th/dot_general | solution.py:78
  142.6 8.4 %fusion.115 = (f32[2,1024]{1,0:T(2,128)S(1)}, f32[2,1024,1024]{1,2,0:T(8,128)}) fusion(pred[1024,1024]{0,1:T(8,128)(4,1)} %iota_compare_fusion, bf16[1024,2,256]{0,2,1:T(8,128)(2,1)} %bitcast.63, bf16[1024,2,256]{0,2,1:T(8,128)(2,1)} %bitcast.60), kind=kOutput, calls=%fused_computation.145 | convolution fusion | flops 1082131456 | bytes 11542528 | tf_op jit(solution)/shard_map/sub | solution.py:73
  151.0 6.3 %fusion.4 = f32[2,256,1024]{2,1,0:T(8,128)} fusion(bf16[1024,2,256]{0,2,1:T(8,128)(2,1)} %bitcast.65, f32[2,1024,1024]{1,2,0:T(8,128)} %get-tuple-element.8, f32[2,1024]{1,0:T(2,128)S(1)} %get-tuple-element.7), kind=kOutput, calls=%fused_computation.14 | convolution fusion | flops 1077936128 | bytes 11542528 | tf_op jit(solution)/shard_map/hqk,khd->qhd/dot_general | solution.py:75
  157.3 0.0 all-gather.7.cloned.1.call-done
  157.3 7.4 %fusion.15 = bf16[1024,2,256]{0,2,1:T(8,128)(2,1)} fusion(f32[2,256,1024]{2,1,0:T(8,128)} %fusion.4, f32[2]{0:T(128)S(1)} %get-tuple-element.5, f32[1024,2]{0,1:T(2,128)S(1)} %fusion.90, f32[2]{0:T(128)S(1)} %get-tuple-element.6, bf16[1024,2,256]{2,0,1:T(8,128)(2,1)} %copy.39, bf16[8,2,256,256]{3,2,1,0:T(8,128)(2,1)} %all-gather.7.cloned.1.call-done, ...), kind=kOutput, calls=%fused_computation.26 | convolution fusion | flops 1621753856 | bytes 7872542 | tf_op jit(solution)/shard_map/thd,hde->the/dot_general | solution.py:77
  164.7 0.0 all-gather.9.cloned.1.call-update
  164.7 4.0 %copy.44 = bf16[512,2048]{0,1:T(8,128)(2,1)} copy(bf16[512,2048]{1,0:T(8,128)(2,1)} %param.10) | data formatting | bytes 4194304 | tf_op args[4]
  168.7 40.1 %all_to_all.25 = bf16[512,4,512]{0,2,1:T(8,128)(2,1)} all-to-all(bf16[512,4,512]{0,2,1:T(8,128)(2,1)} %bitcast.54), channel_id=1, replica_groups=mesh['seq_0'=8,'seq_1'=4,'seq_2'=2,'head'=4] {'head'}, dimensions={1} | all-to-all | bytes 4194304 | tf_op jit(solution)/shard_map/all_to_all | solution.py:82
  208.8 4.2 %copy.45 = bf16[4,512,512]{2,1,0:T(8,128)(2,1)} copy(bf16[4,512,512]{1,2,0:T(8,128)(2,1)} %bitcast.53) | data formatting | bytes 4194304 | tf_op jit(solution)/shard_map/all_to_all | solution.py:82
  213.0 20.6 %all-gather.9.cloned.1.call-done = bf16[1024,2048]{0,1:T(8,128)(2,1)} async-done(((bf16[1024,512]{0,1:T(8,128)(2,1)}), bf16[1024,2048]{0,1:T(8,128)(2,1)}) %all-gather.9.cloned.1.call-update) | async-done | bytes 4194320 | tf_op jit(solution)/shard_map/all_gather | solution.py:84
  233.6 6.2 %convolution_convert_fusion = bf16[1024,512]{1,0:T(8,128)(2,1)} fusion(bf16[1024,2048]{0,1:T(8,128)(2,1)} %all-gather.9.cloned.1.call-done, bf16[2048,512]{1,0:T(8,128)(2,1)} %bitcast.58), kind=kOutput, calls=%fused_computation.29 | convolution fusion | flops 2148007936 | bytes 7340032 | tf_op jit(solution)/shard_map/dot_general | solution.py:83
  (6 shorter events, 0.1 us)
Async XLA Ops:
  6.5 58.5 %copy-start = (bf16[2048,512]{1,0:T(8,128)(2,1)S(1)}, bf16[2048,512]{1,0:T(8,128)(2,1)}, u32[]{:S(2)}) copy-start(bf16[2048,512]{1,0:T(8,128)(2,1)} %param.8) | copy-start | bytes 6291460
  6.5 95.6 %all-gather.5.cloned.1.call-start = ((), (), s32[]{:S(2)}) async-start(), calls=%async_computation.2 | async-start | bytes 1310720 | tf_op jit(solution)/shard_map/all_gather | solution.py:22
  8.7 52.9 %copy-start.3 = (bf16[2048,512]{1,0:T(8,128)(2,1)S(1)}, bf16[2048,512]{1,0:T(8,128)(2,1)}, u32[]{:S(2)}) copy-start(bf16[2048,512]{1,0:T(8,128)(2,1)} %param.9) | copy-start | bytes 6291460
  61.6 3.4 %copy-start.1 = (bf16[4,1024,512]{1,2,0:T(8,128)(2,1)}, bf16[4,1024,512]{1,2,0:T(8,128)(2,1)S(1)}, u32[]{:S(2)}) copy-start(bf16[4,1024,512]{1,2,0:T(8,128)(2,1)S(1)} %all_to_all.24) | copy-start | bytes 12582916
  68.2 1.4 copy-start.2
  69.5 7.3 %copy-start.4 = (f32[2]{0:T(128)S(1)}, f32[2]{0:T(128)}, u32[]{:S(2)}) copy-start(f32[2]{0:T(128)} %param.11) | copy-start | bytes 28
  76.8 80.6 %all-gather.7.cloned.1.call-start = ((), (), s32[]{:S(2)}) async-start(), calls=%async_computation.3 | async-start | bytes 2359296 | tf_op jit(solution)/shard_map/all_gather | solution.py:22
  104.2 129.4 %all-gather.9.cloned.1.call-start = ((), (), s32[]{:S(2)}) async-start(), calls=%async_computation.4 | async-start | bytes 5242880 | tf_op jit(solution)/shard_map/all_gather | solution.py:84
Sparse Core Ops, SparseCore 0:
  76.9 25.1 all-gather.4
  104.3 39.1 all-gather.6
  164.8 68.6 all-gather.8
